TPU v7x, 256 devices: a 2x2x32 block of a 4x8x32 slice. The times are simulated.
256 devices in a mesh: grp: 4 (over y, x), det: 32 (over z), wlk: 2 (over core).
Axes of the slice: x: 2, y: 2, z: 32, core: 2. Of those that a mesh axis runs over, the one named last changes fastest.
The devices are a block of a 4x8x32 slice.
Arguments:
- greens: bfloat16 [256, 450, 150], P(('grp', 'det', 'wlk')), parts along dimension 0, may hold values from -2 to 2
- chol_vectors: bfloat16 [8192, 450, 150], P(('grp', 'det')), parts along dimension 0, may hold values from -0.0234375 to 0.0234375
- hole_orbitals: int32 [16384, 4], P(('grp', 'det')), parts along dimension 0, may hold values from 0 to 63, as said below
- particle_orbitals: int32 [16384, 4], P(('grp', 'det')), parts along dimension 0, may hold values from 0 to 63, as said below
- excitation_order: int32 [16384], P(('grp', 'det')), parts along dimension 0, may hold values from 0 to 4
- amplitudes: float32 [16384], P(('grp', 'det')), parts along dimension 0, may hold values from -0.6 to 0.6
Outputs:
- correlation: float32 [256], P(('grp', 'det', 'wlk')), parts along dimension 0
- force_bias: float32 [256, 2048], P(('grp', 'det', 'wlk')), parts along dimension 0
There are 4 independent parts, one for each index of `grp`. A program takes and returns all parts, laid end to end along the dimension named above; each array names one. Nothing has to cross between parts.
Inputs may be any that keep to these rules, and one draw needn't show every extreme that they name: `hole_orbitals`: within each determinant the 4 entries are distinct. `particle_orbitals`: within each determinant the 4 entries are distinct.
All inputs are finite; a program needn't handle non-finite values.
Results may differ from a plain program's by a relative error of at most 0.00035.
Values may be sent and summed in bfloat16 or wider, within the bound.
A program may use at most 128 MiB of HBM per device.

v0:
```python
import jax
import jax.numpy as jnp
from jax import lax
from jax.sharding import PartitionSpec as P

NOCC = 150
NVIR = 450
NAO = 64
NAV = 64
MAXEXC = 4


def joined_along(pieces, dim):
    pieces = jnp.moveaxis(pieces, 0, dim)
    dims = pieces.shape
    return pieces.reshape(*dims[:dim], dims[dim] * dims[dim + 1], *dims[dim + 2 :])


def sent_to_all(value, axis):
    devices = lax.axis_size(axis)
    return lax.all_to_all(
        jnp.broadcast_to(value[None], (devices, *value.shape)), axis, 0, 0, tiled=True
    )


def gather_directly(value, axis, dim):
    return joined_along(sent_to_all(value, axis), dim)


def minor_determinant(matrix):
    column_pairs = ((0, 1), (0, 2), (0, 3), (1, 2), (1, 3), (2, 3))
    parity = (1.0, -1.0, 1.0, 1.0, -1.0, 1.0)
    result = 0.0
    for number in range(6):
        first_column, second_column = column_pairs[number]
        third_column, fourth_column = column_pairs[5 - number]
        uppers = (
            matrix[0][first_column] * matrix[1][second_column]
            - matrix[1][first_column] * matrix[0][second_column]
        )
        lowers = (
            matrix[2][third_column] * matrix[3][fourth_column]
            - matrix[3][third_column] * matrix[2][fourth_column]
        )
        result = result + parity[number] * uppers * lowers
    return result


def divisor_below(amount, target):
    return max(
        (candidate for candidate in range(1, min(target, amount) + 1) if amount % candidate == 0)
    )


def split_product(form, values, table):
    upper_part = lax.optimization_barrier(values.astype(jnp.bfloat16))
    lower_part = (values - upper_part.astype(jnp.float32)).astype(jnp.bfloat16)
    first = jnp.einsum(form, upper_part, table, preferred_element_type=jnp.float32)
    second = jnp.einsum(form, lower_part, table, preferred_element_type=jnp.float32)
    return first + second


def block_terms(active_green, hole_rows, particle_rows, order_rows, weight_rows):
    particle_hot = (particle_rows[:, :, None] == jnp.arange(NAV)[None, None, :]).astype(
        jnp.bfloat16
    )
    hole_hot = (hole_rows[:, :, None] == jnp.arange(NAO)[None, None, :]).astype(jnp.bfloat16)
    picked_rows = jnp.einsum(
        "dja,wai->wdji", particle_hot, active_green, preferred_element_type=jnp.float32
    ).astype(jnp.bfloat16)
    matrix = jnp.einsum("wdji,dli->jldw", picked_rows, hole_hot, preferred_element_type=jnp.float32)
    positions = jnp.arange(MAXEXC)
    row_live = positions[:, None] < order_rows[None, :]
    live_mask = (row_live[:, None, :] & row_live[None, :, :])[:, :, :, None]
    identity = jnp.eye(MAXEXC, dtype=jnp.float32)[:, :, None, None]
    padded = jnp.where(live_mask, matrix, identity)
    ratios, pullback = jax.vjp(minor_determinant, padded)
    cofactors = pullback(jnp.ones_like(ratios))[0]
    weighted = jnp.where(live_mask, cofactors, 0.0) * weight_rows[None, None, :, None]
    correlation_part = jnp.sum(ratios * weight_rows[:, None], axis=0)
    spread = split_product("jldw,dli->wdji", weighted, hole_hot)
    gradient = split_product("wdji,dja->wai", spread, particle_hot)
    return (gradient, correlation_part)


def det_sums(active_green, hole_orbitals, particle_orbitals, excitation_order, amplitudes):
    walkers = active_green.shape[0]
    det_count = hole_orbitals.shape[0]
    block_size = divisor_below(det_count, max(1, 8192 // walkers))
    blocks = det_count // block_size
    stacked = (
        hole_orbitals.reshape(blocks, block_size, MAXEXC),
        particle_orbitals.reshape(blocks, block_size, MAXEXC),
        excitation_order.reshape(blocks, block_size),
        amplitudes.reshape(blocks, block_size),
    )

    def advance(totals, tables):
        gradient, correlation_part = block_terms(
            active_green, tables[0], tables[1], tables[2], tables[3]
        )
        return ((totals[0] + gradient, totals[1] + correlation_part), None)

    zeros = (jnp.zeros((walkers, NAV, NAO), jnp.float32), jnp.zeros((walkers,), jnp.float32))
    (gradient, correlation_sum), _ = lax.scan(advance, zeros, stacked)
    return (gradient, correlation_sum)


def shards(greens, chol_vectors, hole_orbitals, particle_orbitals, excitation_order, amplitudes):
    offset = NOCC - NAO
    own_walkers = greens.shape[0]
    own_vectors = chol_vectors.shape[0]
    flat_chol = chol_vectors.reshape(own_vectors, NVIR * NOCC)
    walker_piece = lax.all_gather(greens, "det", axis=0, tiled=True)
    flat_piece = walker_piece.reshape(walker_piece.shape[0], NVIR * NOCC)
    whole_term = lax.dot_general(
        flat_piece, flat_chol, (((1,), (1,)), ((), ())), preferred_element_type=jnp.float32
    )
    own_active = greens[:, :NAV, offset:]
    active_chol = chol_vectors[:, :NAV, offset:].reshape(own_vectors, NAV * NAO)
    gathered = gather_directly(own_active.reshape(own_walkers, NAV * NAO), "det", 0)
    group_walkers = gathered.shape[0]
    gradient_part, correlation_part = det_sums(
        gathered.reshape(group_walkers, NAV, NAO),
        hole_orbitals,
        particle_orbitals,
        excitation_order,
        amplitudes,
    )
    gradient_all, correlation_all = lax.psum(
        (gradient_part.reshape(group_walkers, NAV * NAO), correlation_part), "det"
    )
    correlation = 1.0 + lax.dynamic_slice_in_dim(
        correlation_all, lax.axis_index("det") * own_walkers, own_walkers
    )
    gradient_rows = gradient_all.astype(jnp.bfloat16)
    active_term = lax.dot_general(
        gradient_rows, active_chol, (((1,), (1,)), ((), ())), preferred_element_type=jnp.float32
    )
    whole_back, active_back = (
        lax.all_to_all(whole_term, "det", split_axis=0, concat_axis=1, tiled=True),
        lax.all_to_all(active_term, "det", split_axis=0, concat_axis=1, tiled=True),
    )
    force_bias = correlation[:, None] * whole_back + active_back
    return (correlation, force_bias)


def solution(mesh):
    placed = (
        P(("grp", "det", "wlk"), None, None),
        P(("grp", "det"), None, None),
        P(("grp", "det"), None),
        P(("grp", "det"), None),
        P(("grp", "det")),
        P(("grp", "det")),
    )
    return jax.shard_map(
        shards,
        mesh=mesh,
        in_specs=placed,
        out_specs=(P(("grp", "det", "wlk")), P(("grp", "det", "wlk"), None)),
        check_vma=False,
    )
```

profile of v0, /device:TPU:38, one launch (start us, length us, event | category | flops | bytes accessed | tf_op | source)
XLA Modules:
  0.0 317.4 jit_solution(2496577431182868055)
XLA Ops:
  9.1 2.2 reduce.5
  11.3 0.9 reshape.1767
  12.2 32.7 %all-to-all-start = ((bf16[32,2,2048]{2,1,0:T(2,128)(2,1)}), bf16[32,2,2048]{2,1,0:T(2,128)(2,1)S(1)}, u32[]{:S(2)}, u32[]{:S(2)}) async-start(bf16[32,2,2048]{2,1,0:T(2,128)(2,1)} %reshape.1767), calls=%async_computation | async-start | bytes 524288 | tf_op jit(solution)/shard_map/all_to_all | solution.py:21
  46.4 1.3 slice.203
  47.7 1.2 copy.102
  49.0 0.8 reshape.1747
  49.8 36.9 %all-to-all-done = bf16[32,2,2048]{2,1,0:T(2,128)(2,1)S(1)} async-done(((bf16[32,2,2048]{2,1,0:T(2,128)(2,1)}), bf16[32,2,2048]{2,1,0:T(2,128)(2,1)S(1)}, u32[]{:S(2)}, u32[]{:S(2)}) %all-to-all-start) | async-done | bytes 262176 | tf_op jit(solution)/shard_map/all_to_all | solution.py:21
  87.0 1.5 reduce
  89.9 6.4 %copy.94 = bf16[32,128,4,64]{3,0,2,1:T(8,128)(2,1)} copy(bf16[32,128,4,64]{1,3,0,2:T(8,128)(2,1)S(1)} %convert_bitcast_fusion) | data formatting | bytes 4194304 | tf_op jit(solution)/shard_map/while/body/eval_jaxpr/convert_element_type | solution.py:70
  96.3 7.7 %fusion.53 = f32[128,4,32,4]{2,1,3,0:T(4,128)S(1)} fusion(bf16[32,128,4,64]{3,0,2,1:T(8,128)(2,1)} %copy.94, s32[128,4]{1,0:T(8,128)S(1)} %copy.91), kind=kOutput, calls=%fused_computation.173 | convolution fusion | flops 8421376 | bytes 2361344 | tf_op jit(solution)/shard_map/while/body/eval_jaxpr/wdji,dli->jldw/dot_general | solution.py:71
  106.7 1.7 fusion.49
  108.4 5.0 %bitcast_convert_fusion = (bf16[32,128,4,64]{3,0,2,1:T(8,128)(2,1)S(1)}, f32[128,64,4,32]{1,3,2,0:T(8,128)}) fusion(f32[128,64,4,32]{1,3,2,0:T(8,128)S(1)} %fusion.49, bf16[4,4,128,32]{3,1,0,2:T(4,128)(2,1)S(1)} %copy.98, s32[128,4]{1,0:T(8,128)S(1)} %copy.91), kind=kOutput, calls=%fused_computation.1 | convolution fusion | flops 10518528 | bytes 10618880 | tf_op jit(solution)/shard_map/while/body/eval_jaxpr/jldw,dli->wdji/dot_general | solution.py:58
  113.3 0.8 copy-done
  114.1 2.0 copy-done.1
  116.1 2.5 fusion.7
  118.6 11.7 %fusion = bf16[32,128,4,64]{3,0,2,1:T(8,128)(2,1)} fusion(bf16[32,128,4,64]{3,0,2,1:T(8,128)(2,1)} %copy-done.1, f32[128,64,4,32]{1,3,2,0:T(8,128)} %get-tuple-element.135, f32[128,64,4,32]{1,3,2,0:T(8,128)} %copy-done), kind=kLoop, calls=%fused_computation.2 | loop fusion | flops 4194304 | bytes 12582912 | tf_op jit(solution)/shard_map/while/body/eval_jaxpr/convert_element_type | solution.py:57
  130.4 4.8 %fusion.16 = f32[32,64,64]{2,1,0:T(8,128)S(1)} fusion(f32[64,32,64]{2,0,1:T(8,128)S(1)} %fusion.7, bf16[32,128,4,64]{3,0,2,1:T(8,128)(2,1)} %fusion, s32[128,4]{0,1:T(4,128)S(1)} %copy-done.2), kind=kOutput, calls=%fused_computation.13 | convolution fusion | flops 134381568 | bytes 3147776 | tf_op jit(solution)/shard_map/while/body/eval_jaxpr/wdji,dja->wai/dot_general | solution.py:59
  135.7 112.8 %all-reduce.98 = (f32[32]{0:T(128)S(1)}, bf16[32,4096]{1,0:T(8,128)(2,1)S(1)}) all-reduce(f32[32]{0:T(128)S(1)} %fusion.31, f32[32,4096]{1,0:T(8,128)S(1)} %reshape.1746), channel_id=1, replica_groups=mesh['grp'=4,'det'=32,'wlk'=2] {'det'}, use_global_device_ids=true, to_apply=%region_1.2 | all-reduce | flops 131104 | bytes 786688 | tf_op jit(solution)/shard_map/psum | solution.py:130
  248.5 0.9 fusion.68
  249.4 7.3 %all-to-all-start.2 = ((f32[32,1,64]{2,1,0:T(1,128)}), f32[32,1,64]{2,1,0:T(1,128)S(1)}, u32[]{:S(2)}, u32[]{:S(2)}) async-start(f32[32,1,64]{2,1,0:T(1,128)} %bitcast.86), calls=%async_computation.2 | async-start | bytes 32768 | tf_op jit(solution)/shard_map/all_to_all | solution.py:142
  256.7 8.6 %fusion.1 = f32[32,64,1]{1,0,2:T(8,128)} fusion(bf16[64,450,150]{1,0,2:T(8,128)(2,1)} %param.7, bf16[32,450,150]{1,2,0:T(8,128)(2,1)} %all-gather.2.cloned.1.call-done), kind=kOutput, calls=%fused_computation.3 | convolution fusion | flops 276480000 | bytes 12968192 | tf_op jit(solution)/shard_map/dot_general | solution.py:116
  265.3 12.9 %all-to-all-done.2 = f32[32,1,64]{2,1,0:T(1,128)S(1)} async-done(((f32[32,1,64]{2,1,0:T(1,128)}), f32[32,1,64]{2,1,0:T(1,128)S(1)}, u32[]{:S(2)}, u32[]{:S(2)}) %all-to-all-start.2) | async-done | bytes 8224 | tf_op jit(solution)/shard_map/all_to_all | solution.py:142
  278.2 8.9 %all-to-all-start.1 = ((f32[32,1,64]{2,1,0:T(1,128)}), f32[32,1,64]{2,1,0:T(1,128)S(1)}, u32[]{:S(2)}, u32[]{:S(2)}) async-start(f32[32,1,64]{2,1,0:T(1,128)} %bitcast.77), calls=%async_computation.1 | async-start | bytes 32768 | tf_op jit(solution)/shard_map/all_to_all | solution.py:141
  288.3 20.3 %all-to-all-done.1 = f32[32,1,64]{2,1,0:T(1,128)S(1)} async-done(((f32[32,1,64]{2,1,0:T(1,128)}), f32[32,1,64]{2,1,0:T(1,128)S(1)}, u32[]{:S(2)}, u32[]{:S(2)}) %all-to-all-start.1) | async-done | bytes 8224 | tf_op jit(solution)/shard_map/all_to_all | solution.py:141
  (65 shorter events, 9.3 us)
Async XLA Ops:
  7.2 42.6 %copy-start.4 = (s32[128]{0:T(128)S(1)}, s32[128]{0:T(128)}, u32[]{:S(2)}) copy-start(s32[128]{0:T(128)} %param.10) | copy-start | bytes 1540
  9.1 80.0 %copy-start.2 = (s32[128,4]{0,1:T(4,128)S(1)}, s32[128,4]{0,1:T(4,128)}, u32[]{:S(2)}) copy-start(s32[128,4]{0,1:T(4,128)} %param.9) | copy-start | bytes 6148
  12.2 74.6 %all-to-all-start = ((bf16[32,2,2048]{2,1,0:T(2,128)(2,1)}), bf16[32,2,2048]{2,1,0:T(2,128)(2,1)S(1)}, u32[]{:S(2)}, u32[]{:S(2)}) async-start(bf16[32,2,2048]{2,1,0:T(2,128)(2,1)} %reshape.1767), calls=%async_computation | async-start | bytes 524288 | tf_op jit(solution)/shard_map/all_to_all | solution.py:21
  44.8 211.9 %all-gather.2.cloned.1.call-start = ((), (), s32[]{:S(2)}) async-start(), calls=%async_computation.3 | async-start | bytes 5136384 | tf_op jit(solution)/shard_map/all_gather | solution.py:114
  104.0 1.3 copy-start.3
  108.4 5.8 %copy-start = (f32[128,64,4,32]{1,3,2,0:T(8,128)}, f32[128,64,4,32]{1,3,2,0:T(8,128)S(1)}, u32[]{:S(2)}) copy-start(f32[128,64,4,32]{1,3,2,0:T(8,128)S(1)} %fusion.49) | copy-start | bytes 12582916
  114.1 2.0 copy-start.1
  249.4 28.8 %all-to-all-start.2 = ((f32[32,1,64]{2,1,0:T(1,128)}), f32[32,1,64]{2,1,0:T(1,128)S(1)}, u32[]{:S(2)}, u32[]{:S(2)}) async-start(f32[32,1,64]{2,1,0:T(1,128)} %bitcast.86), calls=%async_computation.2 | async-start | bytes 32768 | tf_op jit(solution)/shard_map/all_to_all | solution.py:142
  278.2 30.5 %all-to-all-start.1 = ((f32[32,1,64]{2,1,0:T(1,128)}), f32[32,1,64]{2,1,0:T(1,128)S(1)}, u32[]{:S(2)}, u32[]{:S(2)}) async-start(f32[32,1,64]{2,1,0:T(1,128)} %bitcast.77), calls=%async_computation.1 | async-start | bytes 32768 | tf_op jit(solution)/shard_map/all_to_all | solution.py:141
Sparse Core Ops, SparseCore 0:
  47.5 142.9 all-gather.1
where the time goes:
time: 318 us; the launch traced here: 317 us
  blocking collectives  113 us (36%)
  waiting for transfers between devices  70.8 us (22%)
  starting transfers between devices  49.1 us (15%)
  matrix products  31.8 us (10%)
  local copies, waits for them, and re-layouts  20.3 us (6%)
  other arithmetic  16.3 us (5%)
  between operations  16.3 us (5%)
    psum x1, blocking collectives, shards(): lax.psum((gradient_part.reshape(group_walkers, NAV * NAO), correlation_pa...  113 us
    all_to_all x1, waiting for transfers between devices, sent_to_all(): lax.all_to_all(jnp.broadcast_to(value[None], (devices, *value.shape)), ax...  36.9 us
    all_to_all x1, starting transfers between devices, sent_to_all(): lax.all_to_all(jnp.broadcast_to(value[None], (devices, *value.shape)), ax...  32.7 us
    all_to_all x1, waiting for transfers between devices, shards(): lax.all_to_all(whole_term, 'det', split_axis=0, concat_axis=1, tiled=True)  20.3 us
    all_to_all x1, waiting for transfers between devices, shards(): lax.all_to_all(active_term, 'det', split_axis=0, concat_axis=1, tiled=True)  12.9 us
    convert_element_type x2, other arithmetic, split_product(): lower_part = (values - upper_part.astype(jnp.float32)).astype(jnp.bfloat16)  11.8 us
    all_to_all x1, starting transfers between devices, shards(): lax.all_to_all(whole_term, 'det', split_axis=0, concat_axis=1, tiled=True)  8.88 us
    dot_general x1, matrix products, shards(): lax.dot_general(flat_piece, flat_chol, (((1,), (1,)), ((), ())), preferre...  8.55 us
  transfers between devices with their start and end apart: 4, of which 3 were waited for; matrix products, arithmetic and copies ran while one was open for 19% of the time, Pallas kernels for 0%

commit v1 on v0

v1 whole, which is shorter than its diff:
```python
import functools

import jax
import jax.numpy as jnp
from jax import lax
from jax.experimental import pallas as pl
from jax.experimental.pallas import tpu as pltpu
from jax.sharding import PartitionSpec as P

NOCC = 150
NVIR = 450
NAO = 64
NAV = 64
MAXEXC = 4

MESH = pl.DeviceIdType.MESH
F32 = jnp.float32
BF16 = jnp.bfloat16

ROWS = 160
SENT = 152
LANES = 512
BLOCK = 16
BLOCKS = ROWS // BLOCK
BATCH = 4
CHUNKS = ((0, 32), (32, 32), (64, 32), (96, 32), (128, 24))
LAST_UP = (0, 1)
LAST_DOWN = (2, 3, 4)
STRIDE = 4
SHIFTS = (0, 1, 2, -1)


def minor_determinant(matrix):
    column_pairs = ((0, 1), (0, 2), (0, 3), (1, 2), (1, 3), (2, 3))
    parity = (1.0, -1.0, 1.0, 1.0, -1.0, 1.0)
    result = 0.0
    for number in range(6):
        first_column, second_column = column_pairs[number]
        third_column, fourth_column = column_pairs[5 - number]
        uppers = (
            matrix[0][first_column] * matrix[1][second_column]
            - matrix[1][first_column] * matrix[0][second_column]
        )
        lowers = (
            matrix[2][third_column] * matrix[3][fourth_column]
            - matrix[3][third_column] * matrix[2][fourth_column]
        )
        result = result + parity[number] * uppers * lowers
    return result


def transposed_dot(left, right):
    return lax.dot_general(left, right, (((1,), (1,)), ((), ())), preferred_element_type=F32)


def kernel(
    chips,
    schedule,
    green_ref,
    chol_ref,
    hole_ref,
    particle_ref,
    order_ref,
    amp_ref,
    corr_ref,
    bias_ref,
    raw_chol,
    chol,
    greens,
    total,
    tables,
    gradients,
    table_build,
    active,
    grad_total,
    corr_total,
    whole_rows,
    active_rows,
    message,
    inbox,
    chol_sem,
    ring_send,
    ring_recv,
    table_send,
    table_recv,
    table_send_near,
    table_recv_near,
    grad_send,
    grad_recv,
    grad_send_near,
    grad_recv_near,
    back_send,
    back_recv,
):
    half = chips // 2
    members = chips // STRIDE
    me = lax.axis_index("det")

    def chip(offset):
        return {"det": lax.rem(me + offset + chips, chips)}

    def chol_copy(block):
        start = block * BLOCK
        size = min(BLOCK, NOCC - start)
        return pltpu.make_async_copy(
            chol_ref.at[pl.ds(start, size)], raw_chol.at[pl.ds(start, size)], chol_sem.at[block]
        )

    for block in range(BLOCKS):
        chol_copy(block).start()

    barrier = pltpu.get_barrier_semaphore()
    partners = (1, -1, 2, -2, STRIDE, -STRIDE)
    for offset in partners:
        pl.semaphore_signal(barrier, inc=1, device_id=chip(offset), device_id_type=MESH)

    order = order_ref[...]
    live = lax.broadcasted_iota(jnp.int32, (MAXEXC, order.shape[1]), 0) < order
    table_build[...] = jnp.zeros_like(table_build)
    table_build[0:4, :] = jnp.where(live, hole_ref[...], -1).astype(F32)
    table_build[4:8, :] = jnp.where(live, particle_ref[...], -1).astype(F32)
    amp = amp_ref[...]
    high = amp.astype(BF16).astype(F32)
    middle = (amp - high).astype(BF16).astype(F32)
    table_build[8:9, :] = high
    table_build[9:10, :] = middle
    table_build[10:11, :] = amp - high - middle
    tables[0, 0] = table_build[...].astype(BF16)

    greens[0] = jnp.zeros((ROWS, LANES), BF16)
    greens[0, 0:NOCC, 0:NVIR] = green_ref[...]

    pl.semaphore_wait(barrier, len(partners))

    def hop_copy(buffer, send, recv, up, number):
        source = (number - 1) if up else (members - (number - 1)) % members
        target = number if up else members - number
        return pltpu.make_async_remote_copy(
            src_ref=buffer.at[0, source],
            dst_ref=buffer.at[0, target],
            send_sem=send.at[target],
            recv_sem=recv.at[target],
            device_id=chip(STRIDE if up else -STRIDE),
            device_id_type=MESH,
        )

    def near_copy(buffer, send, recv, place, member):
        return pltpu.make_async_remote_copy(
            src_ref=buffer.at[0, member],
            dst_ref=buffer.at[place, member],
            send_sem=send.at[place, member],
            recv_sem=recv.at[place, member],
            device_id=chip(SHIFTS[place]),
            device_id_type=MESH,
        )

    up_hops = members // 2
    down_hops = members - 1 - up_hops

    def start_spread(buffer, sems):
        send, recv, send_near, recv_near = sems
        hop_copy(buffer, send, recv, True, 1).start()
        if down_hops:
            hop_copy(buffer, send, recv, False, 1).start()
        for place in (1, 2, 3):
            near_copy(buffer, send_near, recv_near, place, 0).start()

    def hop_members(number):
        found = [number] if number <= up_hops else []
        return found + ([members - number] if number <= down_hops else [])

    def take_hop(buffer, sems, number):
        send, recv, send_near, recv_near = sems
        if number <= up_hops:
            hop_copy(buffer, send, recv, True, number).wait_recv()
            if number < up_hops:
                hop_copy(buffer, send, recv, True, number + 1).start()
        if number <= down_hops:
            hop_copy(buffer, send, recv, False, number).wait_recv()
            if number < down_hops:
                hop_copy(buffer, send, recv, False, number + 1).start()
        for member in hop_members(number):
            for place in (1, 2, 3):
                near_copy(buffer, send_near, recv_near, place, member).start()

    def take_near(buffer, sems, member):
        for place in (1, 2, 3):
            near_copy(buffer, sems[2], sems[3], place, member).wait_recv()

    def end_spread(buffer, sems):
        send, recv, send_near, recv_near = sems
        for number in range(1, up_hops + 1):
            hop_copy(buffer, send, recv, True, number).wait_send()
        for number in range(1, down_hops + 1):
            hop_copy(buffer, send, recv, False, number).wait_send()
        for member in range(members):
            for place in (1, 2, 3):
                near_copy(buffer, send_near, recv_near, place, member).wait_send()

    table_sems = (table_send, table_recv, table_send_near, table_recv_near)
    grad_sems = (grad_send, grad_recv, grad_send_near, grad_recv_near)

    def ring_copy(up, step, part):
        start, size = CHUNKS[part]
        if up:
            source, target = step - 1, step
        elif isinstance(step, int):
            source = half + step - 1 if step > 1 else 0
            target = half + step if step < half else half
        else:
            source, target = half + step - 1, half + step
        return pltpu.make_async_remote_copy(
            src_ref=greens.at[source, pl.ds(start, size)],
            dst_ref=greens.at[target, pl.ds(start, size)],
            send_sem=ring_send.at[0 if up else 1, step, part],
            recv_sem=ring_recv.at[0 if up else 1, step, part],
            device_id=chip(1 if up else -1),
            device_id_type=MESH,
        )

    start_spread(tables, table_sems)
    for part in range(len(CHUNKS)):
        ring_copy(True, 1, part).start()
        ring_copy(False, 1, part).start()

    total[...] = jnp.zeros_like(total)
    grad_total[...] = jnp.zeros_like(grad_total)
    corr_total[...] = jnp.zeros_like(corr_total)
    whole_rows[...] = jnp.zeros_like(whole_rows)
    active_rows[...] = jnp.zeros_like(active_rows)

    @pl.loop(1, chips)
    def _(slot):
        greens[slot, SENT:ROWS, :] = jnp.zeros((ROWS - SENT, LANES), BF16)

    shift_rows = lax.broadcasted_iota(jnp.int32, (NAO, ROWS // 2), 0)
    shift_columns = lax.broadcasted_iota(jnp.int32, (NAO, ROWS // 2), 1)
    offset = NOCC - NAO - ROWS // 2
    shift = (shift_columns == shift_rows + offset).astype(F32).astype(BF16)
    active[...] = lax.dot_general(
        shift,
        greens[0, ROWS // 2 : ROWS, 0:128],
        (((1,), (0,)), ((), ())),
        preferred_element_type=F32,
    ).astype(BF16)

    def clean_block(block, static_block):
        start = static_block * BLOCK
        size = min(BLOCK, NOCC - start)
        chol_copy(static_block).wait()
        if size < BLOCK:
            chol[pl.ds(start + size, BLOCK - size)] = jnp.zeros(
                (BLOCK - size, chol.shape[1], LANES), BF16
            )
        full = NVIR // 128 * 128
        chol[pl.ds(start, size), :, 0:full] = raw_chol[pl.ds(start, size), :, 0:full]
        chol[pl.ds(start, size), :, full:LANES] = jnp.zeros(
            (size, chol.shape[1], LANES - full), BF16
        )
        chol[pl.ds(start, size), :, full:NVIR] = raw_chol[pl.ds(start, size), :, full:NVIR]

    vectors = chol.shape[1]

    def add_block(slots, block):
        rows = pl.ds(pl.multiple_of(block * BLOCK, BLOCK), BLOCK)
        left = chol[rows].reshape(BLOCK * vectors, LANES)
        right = jnp.concatenate([greens[slot, rows, :] for slot in slots], axis=0)
        total[...] += transposed_dot(left, right)

    def take_total():
        columns = lax.broadcasted_iota(jnp.int32, (vectors, BATCH * BLOCK), 1)
        kept = jnp.zeros((vectors, BATCH * BLOCK), F32)
        for row in range(BLOCK):
            part = total[pl.ds(row * vectors, vectors), :]
            kept = kept + jnp.where(lax.rem(columns, BLOCK) == row, part, 0.0)
        total[...] = jnp.zeros_like(total)
        turned = kept.T
        return [
            jnp.sum(turned[number * BLOCK : (number + 1) * BLOCK, :], axis=0, keepdims=True)
            for number in range(BATCH)
        ]

    def keep_whole(slots, places):
        del slots
        for place, row in zip(places, take_total()):
            whole_rows[place, :, 0:vectors] = row

    def add_determinants(member):
        table = jnp.concatenate([tables[place, member] for place in range(4)], axis=1).astype(F32)
        width = table.shape[1]
        amplitude = table[8:9] + table[9:10] + table[10:11]
        orbital = lax.broadcasted_iota(jnp.int32, (NAO, width), 0).astype(F32)
        particle_hot = jnp.concatenate(
            [
                jnp.where(orbital == table[4 + row : 5 + row], 1.0, 0.0).astype(BF16)
                for row in range(MAXEXC)
            ],
            axis=1,
        )
        picked = jnp.dot(active[:, 0:NAV], particle_hot, preferred_element_type=F32)
        masks = [orbital == table[column : column + 1] for column in range(MAXEXC)]
        matrix = []
        for row in range(MAXEXC):
            own = picked[:, row * width : (row + 1) * width]
            entries = [
                jnp.sum(jnp.where(masks[column], own, 0.0), axis=0, keepdims=True)
                for column in range(MAXEXC)
            ]
            entries[row] = jnp.where(table[4 + row : 5 + row] < 0.0, 1.0, entries[row])
            matrix.append(entries)
        ratios, pullback = jax.vjp(minor_determinant, matrix)
        cofactors = pullback(jnp.ones_like(ratios))[0]
        corr_total[...] += ratios * amplitude
        uppers, lowers = [], []
        for row in range(MAXEXC):
            spread = jnp.zeros((NAO, width), F32)
            for column in range(MAXEXC):
                spread = jnp.where(masks[column], cofactors[row][column] * amplitude, spread)
            upper = spread.astype(BF16)
            uppers.append(upper)
            lowers.append((spread - upper.astype(F32)).astype(BF16))
        spread_all = jnp.concatenate(
            [jnp.concatenate(uppers, axis=1), jnp.concatenate(lowers, axis=1)], axis=0
        )
        grad_total[:, 0:NAV] += transposed_dot(spread_all, particle_hot)

    def finish_gradient():
        whole = grad_total[0:NAO, :] + grad_total[NAO : 2 * NAO, :]
        packed = whole[0 : NAO // 2] + pltpu.roll(whole[NAO // 2 : NAO], NAV, 1)
        gradients[0, 0] = packed.astype(BF16)

    def add_active(member):
        lanes = lax.broadcasted_iota(jnp.int32, (NAO // 2, 128), 1)
        unpacked = []
        for place in range(4):
            packed = gradients[place, member].astype(F32)
            unpacked.append(
                (
                    jnp.where(lanes < NAV, packed, 0.0).astype(BF16),
                    jnp.where(lanes < NAV, pltpu.roll(packed, NAV, 1), 0.0).astype(BF16),
                )
            )
        for block in range(NAO // BLOCK):
            start = NOCC - NAO + block * BLOCK
            left = chol[pl.ds(start, BLOCK), :, 0:128].reshape(BLOCK * vectors, 128)
            side, inner = divmod(block * BLOCK, NAO // 2)
            right = jnp.concatenate(
                [unpacked[place][side][inner : inner + BLOCK] for place in range(4)], axis=0
            )
            total[...] += transposed_dot(left, right)
        for place, row in enumerate(take_total()):
            index = (SHIFTS[place] + STRIDE * member) % chips
            active_rows[index, :, 0:vectors] = row

    events = {}
    for step, action in schedule:
        events.setdefault(step, []).append(action)

    def run_event(action):
        kind, number = action
        if kind == "table_hop":
            take_hop(tables, table_sems, number)
        elif kind == "determinants":
            take_near(tables, table_sems, number)
            add_determinants(number)
        elif kind == "gradient":
            finish_gradient()
            start_spread(gradients, grad_sems)
        elif kind == "grad_hop":
            take_hop(gradients, grad_sems, number)

    def forward(step, part, up, down):
        ring_copy(True, step, part).wait_recv()
        if up:
            ring_copy(True, step + 1, part).start()
        ring_copy(False, step, part).wait_recv()
        if down:
            ring_copy(False, step + 1, part).start()

    for step in (1, 2):
        for part in range(len(CHUNKS)):
            forward(step, part, True, True)
            block = (step - 1) * len(CHUNKS) + part
            clean_block(block, block)
        for action in events.get(step, ()):
            run_event(action)

    @pl.loop(3, half - 1)
    def _(step):
        pair = lax.div(step - 1, 2)
        second = lax.rem(step - 1, 2)
        places = (2 * pair - 1, 2 * pair, half + 2 * pair - 1, half + 2 * pair)
        for part in range(len(CHUNKS)):
            forward(step, part, True, True)
            add_block(places, second * len(CHUNKS) + part)

        @pl.when(second == 1)
        def _():
            keep_whole(places, (places[0], places[1], chips + 1 - 2 * pair, chips - 2 * pair))

        for when, actions in events.items():
            if 3 <= when < half - 1:

                @pl.when(step == when)
                def _(actions=actions):
                    for action in actions:
                        run_event(action)

    step = half - 1
    places = (half - 3, half - 2, 2 * half - 3, 2 * half - 2)
    for part in range(len(CHUNKS)):
        forward(step, part, part in LAST_UP, part in LAST_DOWN)
        for block in (2 * part, 2 * part + 1):
            add_block(places, block)
    keep_whole(places, (half - 3, half - 2, half + 3, half + 2))
    for action in events.get(step, ()):
        run_event(action)

    for member in range(members):
        if member != members // 2:
            if member:
                pass
            take_near(gradients, grad_sems, member)
            add_active(member)
    take_near(gradients, grad_sems, members // 2)
    add_active(members // 2)

    places = (half - 1, 2 * half - 1, half, 0)
    for part in range(len(CHUNKS)):
        if part in LAST_UP:
            ring_copy(True, half, part).wait_recv()
        else:
            ring_copy(False, half, part).wait_recv()
        for block in (2 * part, 2 * part + 1):
            add_block(places, block)
    keep_whole(places, (half - 1, half + 1, half, 0))

    message[...] = whole_rows[...] + pltpu.roll(active_rows[...], vectors, 2)

    def back_copy(offset):
        return pltpu.make_async_remote_copy(
            src_ref=message.at[offset],
            dst_ref=inbox.at[lax.rem(me, 2), lax.div(me, 2)],
            send_sem=back_send.at[offset],
            recv_sem=back_recv.at[offset],
            device_id={"det": lax.rem(me - offset + chips, chips)},
            device_id_type=MESH,
        )

    for offset in range(chips // 2, chips):
        back_copy(offset).start()
        if 0 < chips - offset < chips // 2:
            back_copy(chips - offset).start()
    inbox[lax.rem(me, 2), lax.div(me, 2)] = message[0]

    corr = 1.0 + jnp.sum(corr_total[...], axis=1, keepdims=True)
    corr_ref[...] = jnp.broadcast_to(corr, corr_ref.shape)

    end_spread(tables, table_sems)
    end_spread(gradients, grad_sems)

    for part in range(len(CHUNKS)):
        ring_copy(True, 1, part).wait_send()
        ring_copy(False, 1, part).wait_send()

    @pl.loop(2, half)
    def _(step):
        for part in range(len(CHUNKS)):
            ring_copy(True, step, part).wait_send()
            ring_copy(False, step, part).wait_send()

    for part in LAST_UP:
        ring_copy(True, half, part).wait_send()
    for part in LAST_DOWN:
        ring_copy(False, half, part).wait_send()

    for offset in range(1, chips):
        back_copy(offset).wait_send()

    def back_wait(offset):
        sender = lax.rem(me + offset, chips)
        pltpu.make_async_remote_copy(
            src_ref=message.at[offset],
            dst_ref=inbox.at[lax.rem(sender, 2), lax.div(sender, 2)],
            send_sem=back_send.at[offset],
            recv_sem=back_recv.at[offset],
            device_id=chip(offset),
            device_id_type=MESH,
        ).wait_recv()

    for offset in range(1, chips):
        back_wait(offset)

    even = inbox[0].reshape(chips // 2, 128)
    odd = inbox[1].reshape(chips // 2, 128)
    lanes = lax.broadcasted_iota(jnp.int32, even.shape, 1)
    even = corr * even + pltpu.roll(even, vectors, 1)
    odd = corr * pltpu.roll(odd, vectors, 1) + odd
    bias_ref[...] = jnp.where(lanes < vectors, even, odd)


def plan(chips):
    return (
        (2, ("table_hop", 1)),
        (3, ("determinants", 0)),
        (3, ("table_hop", 2)),
        (4, ("determinants", 1)),
        (4, ("determinants", 7)),
        (5, ("table_hop", 3)),
        (6, ("determinants", 2)),
        (6, ("determinants", 6)),
        (6, ("table_hop", 4)),
        (7, ("determinants", 3)),
        (7, ("determinants", 5)),
        (8, ("determinants", 4)),
        (8, ("gradient", 0)),
        (10, ("grad_hop", 1)),
        (12, ("grad_hop", 2)),
        (13, ("grad_hop", 3)),
        (15, ("grad_hop", 4)),
    )


def shards(greens, chol_vectors, hole_orbitals, particle_orbitals, excitation_order, amplitudes):
    chips = lax.axis_size("det")
    vectors = chol_vectors.shape[0]
    dets = hole_orbitals.shape[0]
    members = chips // STRIDE
    half = chips // 2
    dma = pltpu.SemaphoreType.DMA
    vmem = pl.BlockSpec(memory_space=pltpu.VMEM)
    corr, bias = pl.pallas_call(
        functools.partial(kernel, chips, plan(chips)),
        out_shape=(
            jax.ShapeDtypeStruct((1, 128), F32),
            jax.ShapeDtypeStruct((chips * vectors // 128, 128), F32),
        ),
        in_specs=[vmem, pl.BlockSpec(memory_space=pl.ANY), vmem, vmem, vmem, vmem],
        out_specs=(vmem, vmem),
        scratch_shapes=[
            pltpu.VMEM((NOCC, vectors, NVIR), BF16),
            pltpu.VMEM((ROWS, vectors, LANES), BF16),
            pltpu.VMEM((chips, ROWS, LANES), BF16),
            pltpu.VMEM((BLOCK * vectors, BATCH * BLOCK), F32),
            pltpu.VMEM((4, members, 16, dets), BF16),
            pltpu.VMEM((4, members, NAO // 2, 128), BF16),
            pltpu.VMEM((16, dets), F32),
            pltpu.VMEM((NAO, 128), BF16),
            pltpu.VMEM((2 * NAO, 128), F32),
            pltpu.VMEM((1, 4 * dets), F32),
            pltpu.VMEM((chips, 1, 128), F32),
            pltpu.VMEM((chips, 1, 128), F32),
            pltpu.VMEM((chips, 1, 128), F32),
            pltpu.VMEM((2, half, 1, 128), F32),
            dma((BLOCKS,)),
            dma((2, half + 1, len(CHUNKS))),
            dma((2, half + 1, len(CHUNKS))),
            dma((members,)),
            dma((members,)),
            dma((4, members)),
            dma((4, members)),
            dma((members,)),
            dma((members,)),
            dma((4, members)),
            dma((4, members)),
            dma((chips,)),
            dma((chips,)),
        ],
        compiler_params=pltpu.CompilerParams(
            collective_id=0, has_side_effects=True, vmem_limit_bytes=56 * 1024 * 1024
        ),
        name="walker_ring",
    )(
        jnp.transpose(greens, (0, 2, 1)).reshape(NOCC, NVIR),
        jnp.transpose(chol_vectors, (2, 0, 1)),
        jnp.transpose(hole_orbitals),
        jnp.transpose(particle_orbitals),
        excitation_order.reshape(1, dets),
        amplitudes.reshape(1, dets),
    )
    return (corr[0, 0:1], bias.reshape(1, chips * vectors))


def solution(mesh):
    placed = (
        P(("grp", "det", "wlk"), None, None),
        P(("grp", "det"), None, None),
        P(("grp", "det"), None),
        P(("grp", "det"), None),
        P(("grp", "det")),
        P(("grp", "det")),
    )
    return jax.shard_map(
        shards,
        mesh=mesh,
        in_specs=placed,
        out_specs=(P(("grp", "det", "wlk")), P(("grp", "det", "wlk"), None)),
        check_vma=False,
    )
```

time: 318 us -> 123 us (0.39)
  Pallas kernels: 0 us -> 119 us
  blocking collectives: 113 us -> 0 us
  waiting for transfers between devices: 70.8 us -> 0 us
  starting transfers between devices: 49.1 us -> 0 us
  matrix products: 31.8 us -> 0 us
  local copies, waits for them, and re-layouts: 20.3 us -> 1.3 us
  other arithmetic: 16.3 us -> 0 us
  between operations: 16.3 us -> 2.4 us
    pallas_call x0 -> x1, Pallas kernels: none -> 119 us  [shards(): pl.pallas_call(functools.partial(kernel, chips, plan(chips)), out_shape=(...]
    psum x1 -> x0, blocking collectives: 113 us -> none  [shards(): lax.psum((gradient_part.reshape(group_walkers, NAV * NAO), correlation_pa...]
    all_to_all x3 -> x0, waiting for transfers between devices: 70.2 us -> none  [the longest x1 36.9 us: sent_to_all(): lax.all_to_all(jnp.broadcast_to(value[None], (devices, *value.shape)), ax...]
    all_to_all x3 -> x0, starting transfers between devices: 48.9 us -> none  [the longest x1 32.7 us: sent_to_all(): lax.all_to_all(jnp.broadcast_to(value[None], (devices, *value.shape)), ax...]
    dot_general x8 -> x0, matrix products: 31.8 us -> none  [the longest x1 8.55 us: shards(): lax.dot_general(flat_piece, flat_chol, (((1,), (1,)), ((), ())), preferre...]
    convert_element_type x4 -> x0, other arithmetic: 12.2 us -> none  [the longest x2 11.8 us: split_product(): lower_part = (values - upper_part.astype(jnp.float32)).astype(jnp.bfloat16)]
    convert_element_type x2 -> x0, local copies, waits for them, and re-layouts: 6.87 us -> none  [the longest x1 6.43 us: block_terms(): picked_rows = jnp.einsum('dja,wai->wdji', particle_hot, active_green, pre...]
    unnamed x13 -> x1, local copies, waits for them, and re-layouts: 4.75 us -> 1.3 us
  transfers between devices with their start and end apart: 4 -> 0, of which waited for: 3 -> 0; matrix products, arithmetic and copies ran while one was open for 19% -> 0% of each run, Pallas kernels for 0% -> 0%
where the time goes in v1:
time: 123 us
  Pallas kernels  119 us (97%)
  between operations  2.4 us (2%)
  local copies, waits for them, and re-layouts  1.3 us (1%)
    pallas_call x1, Pallas kernels, shards(): pl.pallas_call(functools.partial(kernel, chips, plan(chips)), out_shape=(...  119 us

profile of v1, /device:TPU:38, one launch (start us, length us, event | category | flops | bytes accessed | tf_op | source)
XLA Modules:
  0.0 122.6 jit_solution(13496372208747913448)
XLA Ops:
  0.6 118.9 %walker_ring.1 = (f32[1,128]{1,0:T(1,128)}, f32[16,128]{1,0:T(8,128)}) custom-call(bf16[150,450]{1,0:T(8,128)(2,1)} %bitcast.12, bf16[150,64,450]{2,1,0:T(8,128)(2,1)} %bitcast.11, s32[4,128]{1,0:T(4,128)} %bitcast.14, s32[4,128]{1,0:T(4,128)} %bitcast.15, s32[1,128]{1,0:T(1,128)} %bitcast.16, f32[1,128]{1,0:T(1,128)} %bitcast.17), custom_call_target="tpu_custom_call" | custom-call | tf_op jit(solution)/shard_map/walker_ring/pallas_call | solution.py:532
  120.2 1.3 %copy.11 = f32[1,2048]{1,0:T(1,128)} copy(f32[1,2048]{1,0:T(1,128)} %bitcast.13) | data formatting | bytes 16384

commit v2 on v0

v2 whole, which is shorter than its diff:
```python
import functools

import jax
import jax.numpy as jnp
from jax import lax
from jax.experimental import pallas as pl
from jax.experimental.pallas import tpu as pltpu
from jax.sharding import PartitionSpec as P

NOCC = 150
NVIR = 450
NAO = 64
NAV = 64
MAXEXC = 4

MESH = pl.DeviceIdType.MESH
F32 = jnp.float32
BF16 = jnp.bfloat16

ROWS = 160
SENT = 152
LANES = 512
BLOCK = 16
BLOCKS = ROWS // BLOCK
BATCH = 8
FULL = NVIR // 128 * 128
PART = 64
SPARE = NOCC - ROWS // 2
LAST = (NVIR - FULL - PART, -(-NOCC // PART))
CHUNKS = (
    (1, 80, 72, 384),
    (0, 80, 72, 384),
    (1, 0, 48, 512),
    (0, 0, 48, 512),
    (1, 48, 32, 512),
    (0, 48, 32, 512),
)
LAST_UP = (0, 2, 4)
LAST_DOWN = (1, 3, 5)
CLEANED = {(1, 1): 0, (1, 2): 1, (1, 4): 2, (2, 0): 3, (2, 2): 4}
HALF_BLOCKS = ((0,), (1,), (2,), (3,), (4,), ())
ALL_BLOCKS = ((0, 1), (2,), (3, 4), (5,), (6, 7), (8, 9))
LAST_BLOCKS = ((), (5, 6, 7, 8, 9), (), (0, 1, 2), (), (3, 4))
STRIDE = 4
SHIFTS = (0, 1, 2, -1)


def minor_determinant(matrix):
    column_pairs = ((0, 1), (0, 2), (0, 3), (1, 2), (1, 3), (2, 3))
    parity = (1.0, -1.0, 1.0, 1.0, -1.0, 1.0)
    result = 0.0
    for number in range(6):
        first_column, second_column = column_pairs[number]
        third_column, fourth_column = column_pairs[5 - number]
        uppers = (
            matrix[0][first_column] * matrix[1][second_column]
            - matrix[1][first_column] * matrix[0][second_column]
        )
        lowers = (
            matrix[2][third_column] * matrix[3][fourth_column]
            - matrix[3][third_column] * matrix[2][fourth_column]
        )
        result = result + parity[number] * uppers * lowers
    return result


def transposed_dot(left, right):
    return lax.dot_general(left, right, (((1,), (1,)), ((), ())), preferred_element_type=F32)


def kernel(
    chips,
    green_ref,
    chol_ref,
    hole_ref,
    particle_ref,
    order_ref,
    amp_ref,
    corr_ref,
    bias_ref,
    raw_chol,
    chol,
    active_chol,
    greens,
    total,
    tables,
    gradients,
    table_build,
    peer_rows,
    active,
    grad_total,
    corr_total,
    message,
    inbox,
    peer_inbox,
    corr_out,
    corr_in,
    pack,
    leftover,
    chol_sem,
    swap_send,
    swap_recv,
    ring_send,
    ring_recv,
    table_send,
    table_recv,
    table_send_near,
    table_recv_near,
    grad_send,
    grad_recv,
    grad_send_near,
    grad_recv_near,
    back_send,
    back_recv,
):
    half = chips // 2
    members = chips // STRIDE
    vectors = chol.shape[1]
    me = lax.axis_index("det")
    core = lax.axis_index("wlk")
    barrier = pltpu.get_barrier_semaphore()

    def chip(offset):
        return {"det": lax.rem(me + offset + chips, chips)}

    def greet(offsets, other):
        for offset in offsets:
            pl.semaphore_signal(barrier, inc=1, device_id=chip(offset), device_id_type=MESH)
        pl.semaphore_signal(barrier, inc=1, device_id={"wlk": other}, device_id_type=MESH)

    def swap_copy(source, target, number, other):
        return pltpu.make_async_remote_copy(
            src_ref=source,
            dst_ref=target,
            send_sem=swap_send.at[number],
            recv_sem=swap_recv.at[number],
            device_id={"wlk": other},
            device_id_type=MESH,
        )

    def block_to_upper(part):
        _, start, size, lanes = CHUNKS[part]
        block = greens.at[0, 0, pl.ds(start, size), pl.ds(0, lanes)]
        return swap_copy(block, block, 4 + part // 2, 1)

    def rows_to_lower():
        rows = greens.at[0, 1, pl.ds(ROWS // 2, ROWS // 2), pl.ds(0, 128)]
        return swap_copy(rows, peer_rows, 1, 0)

    def inbox_swap(other):
        return swap_copy(inbox, peer_inbox, 2, other)

    def corr_to_upper():
        return swap_copy(corr_out, corr_in, 3, 1)

    def back_copy(offset):
        return pltpu.make_async_remote_copy(
            src_ref=message.at[offset],
            dst_ref=inbox.at[lax.rem(me, 2), lax.div(me, 2)],
            send_sem=back_send.at[offset],
            recv_sem=back_recv.at[offset],
            device_id={"det": lax.rem(me - offset + chips, chips)},
            device_id_type=MESH,
        )

    def back_wait(offset):
        sender = lax.rem(me + offset, chips)
        pltpu.make_async_remote_copy(
            src_ref=message.at[offset],
            dst_ref=inbox.at[lax.rem(sender, 2), lax.div(sender, 2)],
            send_sem=back_send.at[offset],
            recv_sem=back_recv.at[offset],
            device_id=chip(offset),
            device_id_type=MESH,
        ).wait_recv()

    def take_total():
        columns = lax.broadcasted_iota(jnp.int32, (vectors, BATCH * BLOCK), 1)
        kept = jnp.zeros((vectors, BATCH * BLOCK), F32)
        for row in range(BLOCK):
            part = total[pl.ds(row * vectors, vectors), :]
            kept = kept + jnp.where(lax.rem(columns, BLOCK) == row, part, 0.0)
        total[...] = jnp.zeros_like(total)
        turned = kept.T
        return [
            jnp.sum(turned[number * BLOCK : (number + 1) * BLOCK, :], axis=0, keepdims=True)
            for number in range(BATCH)
        ]

    def keep_rows(places):
        rows = take_total()
        for number, place in enumerate(places):
            message[place] = jnp.concatenate([rows[2 * number], rows[2 * number + 1]], axis=1)

    def own_walker(index):
        greens[0, index] = jnp.zeros((ROWS, LANES), BF16)
        greens[0, index, 0:NOCC, 0:NVIR] = green_ref[...]
        tile = greens[0, index, :, FULL:LANES].astype(F32)
        middle = ROWS // 2
        lanes = lax.broadcasted_iota(jnp.int32, tile.shape, 1)
        rows = lax.broadcasted_iota(jnp.int32, tile.shape, 0)
        further = pltpu.roll(tile[middle:], PART, 1)
        packed = jnp.where(lanes[:middle] < PART, tile[:middle], further)
        for column in range(LAST[0]):
            for third in range(LAST[1]):
                match = (lanes == rows + (1 - third) * PART) & (lanes >= PART)
                row = jnp.sum(
                    jnp.where(match, tile[:, PART + column : PART + column + 1], 0.0),
                    axis=0,
                    keepdims=True,
                )
                place = SPARE + LAST[1] * column + third
                packed = jnp.where(
                    (rows[:middle] == place) & (lanes[:middle] >= PART), row, packed
                )
        greens[0, index, 0:middle, FULL:LANES] = packed.astype(BF16)
        greens[0, index, middle:ROWS, FULL:LANES] = jnp.zeros((middle, LANES - FULL), BF16)

    def write_bias(corr, whole, term, upper):
        even = corr * whole[0].reshape(half, 128) + term[0].reshape(half, 128)
        odd = corr * whole[1].reshape(half, 128) + term[1].reshape(half, 128)
        lanes = lax.broadcasted_iota(jnp.int32, even.shape, 1)
        if upper:
            even = pltpu.roll(even, vectors, 1)
        else:
            odd = pltpu.roll(odd, vectors, 1)
        bias_ref[...] = jnp.where(lanes < vectors, even, odd)
        corr_ref[...] = jnp.broadcast_to(corr, corr_ref.shape)

    def ring_copy(up, step, part):
        walker, start, size, lanes = CHUNKS[part]
        if up:
            source, target = step - 1, step
        elif isinstance(step, int):
            source = half + step - 1 if step > 1 else 0
            target = half + step if step < half else half
        else:
            source, target = half + step - 1, half + step
        return pltpu.make_async_remote_copy(
            src_ref=greens.at[source, walker, pl.ds(start, size), pl.ds(0, lanes)],
            dst_ref=greens.at[target, walker, pl.ds(start, size), pl.ds(0, lanes)],
            send_sem=ring_send.at[0 if up else 1, step, part],
            recv_sem=ring_recv.at[0 if up else 1, step, part],
            device_id=chip(1 if up else -1),
            device_id_type=MESH,
        )

    def chol_copy(block):
        start = block * BLOCK
        size = min(BLOCK, NOCC - start)
        return pltpu.make_async_copy(
            chol_ref.at[pl.ds(start, size)], raw_chol.at[pl.ds(start, size)], chol_sem.at[block]
        )

    def packing():
        rows = lax.broadcasted_iota(jnp.int32, pack.shape, 0)
        columns = lax.broadcasted_iota(jnp.int32, pack.shape, 1)
        within = lax.rem(columns, 128)
        last = PART + jnp.where(within < PART, 1, 0)
        source = jnp.where(
            columns < 128,
            jnp.where(columns < PART, columns, columns + 128 - PART),
            jnp.where(columns < 256, last, last + 128),
        )
        pack[...] = jnp.where(rows == source, 1.0, 0.0).astype(BF16)

    def clean_pair(pair):
        low = pair * BLOCK
        high = ROWS // 2 + low
        size = min(BLOCK, NOCC - high)
        chol_copy(pair).wait()
        chol_copy(pair + BLOCKS // 2).wait()
        tiles = []
        for start, count in ((low, BLOCK), (high, size)):
            block = pl.ds(start, BLOCK)
            if count < BLOCK:
                chol[pl.ds(start + count, BLOCK - count)] = jnp.zeros(
                    (BLOCK - count, vectors, LANES), BF16
                )
            chol[pl.ds(start, count), :, 0:FULL] = raw_chol[pl.ds(start, count), :, 0:FULL]
            chol[block, :, FULL:LANES] = jnp.zeros((BLOCK, vectors, LANES - FULL), BF16)
            chol[pl.ds(start, count), :, FULL:NVIR] = raw_chol[pl.ds(start, count), :, FULL:NVIR]
            tiles.append(chol[block, :, FULL:LANES].reshape(BLOCK * vectors, LANES - FULL))
        made = jnp.dot(
            jnp.concatenate(tiles, axis=1), pack[...], preferred_element_type=F32
        )
        chol[pl.ds(low, BLOCK), :, FULL:LANES] = (
            made[:, 0:128].astype(BF16).reshape(BLOCK, vectors, LANES - FULL)
        )
        chol[pl.ds(high, BLOCK), :, FULL:LANES] = jnp.zeros((BLOCK, vectors, LANES - FULL), BF16)
        within = lax.rem(lax.broadcasted_iota(jnp.int32, (vectors, 128), 1), PART)
        for third in range(LAST[1]):
            found = [
                (row, first)
                for base, first in ((low, 128), (high, 256))
                for row in range(BLOCK)
                if base + row < NOCC and (base + row) // PART == third
            ]
            if found:
                kept = leftover[third]
                for row, first in found:
                    index = (row + (low if first == 128 else high)) % PART
                    part = made[row * vectors : (row + 1) * vectors, first : first + 128]
                    kept = jnp.where(within == index, part, kept)
                leftover[third] = kept

    def place_leftover():
        lanes = lax.broadcasted_iota(jnp.int32, (vectors, 128), 1)
        for third in range(LAST[1]):
            for column in range(LAST[0]):
                row = SPARE + LAST[1] * column + third
                value = leftover[third]
                if column:
                    value = pltpu.roll(value, PART, 1)
                old = chol[row, :, FULL:LANES].astype(F32)
                chol[row, :, FULL:LANES] = jnp.where(lanes < PART, old, value).astype(BF16)

    def add_block(slots, block):
        rows = pl.ds(pl.multiple_of(block * BLOCK, BLOCK), BLOCK)
        left = chol[rows].reshape(BLOCK * vectors, LANES)
        right = jnp.concatenate(
            [greens[slot, walker, rows, :] for slot in slots for walker in range(2)], axis=0
        )
        total[...] += transposed_dot(left, right)

    def forward(step, part, up, down):
        ring_copy(True, step, part).wait_recv()
        if up:
            ring_copy(True, step + 1, part).start()
        ring_copy(False, step, part).wait_recv()
        if down:
            ring_copy(False, step + 1, part).start()

    def upper_core():
        greet((1, -1), 0)
        for block in range(BLOCKS // 2):
            chol_copy(block).start()
            chol_copy(block + BLOCKS // 2).start()
        own_walker(1)
        pl.semaphore_wait(barrier, 3)
        rows_to_lower().start()
        for part in LAST_UP + LAST_DOWN:
            if part in LAST_DOWN:
                block_to_upper(part).wait_recv()
            ring_copy(True, 1, part).start()
            ring_copy(False, 1, part).start()

        total[...] = jnp.zeros_like(total)
        leftover[...] = jnp.zeros_like(leftover)
        packing()

        @pl.loop(1, chips)
        def _(slot):
            for walker in range(2):
                greens[slot, walker, SENT:ROWS, 0:FULL] = jnp.zeros((ROWS - SENT, FULL), BF16)
                greens[slot, walker, ROWS // 2 : ROWS, FULL:LANES] = jnp.zeros(
                    (ROWS // 2, LANES - FULL), BF16
                )

        greens[0, 0, SENT:ROWS, 0:FULL] = jnp.zeros((ROWS - SENT, FULL), BF16)
        greens[0, 0, ROWS // 2 : ROWS, FULL:LANES] = jnp.zeros((ROWS // 2, LANES - FULL), BF16)

        for step in (1, 2):
            for part in range(len(CHUNKS)):
                forward(step, part, True, True)
                if (step, part) in CLEANED:
                    clean_pair(CLEANED[step, part])
        place_leftover()

        @pl.loop(3, half - 1)
        def _(step):
            pair = lax.div(step - 1, 2)
            second = lax.rem(step - 1, 2)
            slots = (2 * pair - 1, 2 * pair, half + 2 * pair - 1, half + 2 * pair)
            for part in range(len(CHUNKS)):
                forward(step, part, True, True)
                for block in HALF_BLOCKS[part]:
                    add_block(slots, second * (BLOCKS // 2) + block)

            @pl.when(second == 1)
            def _():
                places = (slots[0], slots[1], chips + 1 - 2 * pair, chips - 2 * pair)
                keep_rows(places)
                for place in places:
                    back_copy(place).start()

        step = half - 1
        slots = (half - 3, half - 2, 2 * half - 3, 2 * half - 2)
        for part in range(len(CHUNKS)):
            forward(step, part, part in LAST_UP, part in LAST_DOWN)
            for block in ALL_BLOCKS[part]:
                add_block(slots, block)
        places = (half - 3, half - 2, half + 3, half + 2)
        keep_rows(places)
        for place in places:
            back_copy(place).start()

        slots = (half, half - 1, 2 * half - 1, 0)
        for part in range(len(CHUNKS)):
            ring_copy(part in LAST_UP, half, part).wait_recv()
            for block in LAST_BLOCKS[part]:
                add_block(slots, block)
        keep_rows((half, half - 1, half + 1, 0))
        for place in (half, half - 1, half + 1):
            back_copy(place).start()
        inbox[lax.rem(me, 2), lax.div(me, 2)] = message[0]

        rows_to_lower().wait_send()
        for part in range(len(CHUNKS)):
            ring_copy(True, 1, part).wait_send()
            ring_copy(False, 1, part).wait_send()

        @pl.loop(2, half)
        def _(step):
            for part in range(len(CHUNKS)):
                ring_copy(True, step, part).wait_send()
                ring_copy(False, step, part).wait_send()

        for part in range(len(CHUNKS)):
            ring_copy(part in LAST_UP, half, part).wait_send()
        corr_to_upper().wait_recv()
        inbox_swap(0).wait_recv()
        for offset in range(1, chips):
            back_copy(offset).wait_send()
        for offset in range(1, chips):
            back_wait(offset)
        inbox_swap(0).start()
        write_bias(corr_in[1:2, 0:1], inbox[...], peer_inbox[...], True)
        inbox_swap(0).wait_send()

    up_hops = members // 2
    down_hops = members - 1 - up_hops

    def hop_copy(buffer, send, recv, up, number):
        source = (number - 1) if up else (members - (number - 1)) % members
        target = number if up else members - number
        return pltpu.make_async_remote_copy(
            src_ref=buffer.at[0, source],
            dst_ref=buffer.at[0, target],
            send_sem=send.at[target],
            recv_sem=recv.at[target],
            device_id=chip(STRIDE if up else -STRIDE),
            device_id_type=MESH,
        )

    both_ways = (2, members // 2)

    def shift_of(place, member):
        return -SHIFTS[place] if place == 2 and member >= members // 2 else SHIFTS[place]

    def member_of(place, member):
        return 0 if (place, member) == both_ways else member

    def near_copy(buffer, send, recv, place, member):
        return pltpu.make_async_remote_copy(
            src_ref=buffer.at[0, member_of(place, member)],
            dst_ref=buffer.at[place, member],
            send_sem=send.at[place, member],
            recv_sem=recv.at[place, member],
            device_id=chip(shift_of(place, member)),
            device_id_type=MESH,
        )

    def start_spread(buffer, sems):
        send, recv, send_near, recv_near = sems
        hop_copy(buffer, send, recv, True, 1).start()
        if down_hops:
            hop_copy(buffer, send, recv, False, 1).start()
        for place in (1, 2, 3):
            near_copy(buffer, send_near, recv_near, place, 0).start()
        near_copy(buffer, send_near, recv_near, *both_ways).start()

    def hop_members(number):
        found = [number] if number <= up_hops else []
        return found + ([members - number] if number <= down_hops else [])

    def take_hop(buffer, sems, number):
        send, recv, send_near, recv_near = sems
        if number <= up_hops:
            hop_copy(buffer, send, recv, True, number).wait_recv()
            if number < up_hops:
                hop_copy(buffer, send, recv, True, number + 1).start()
        if number <= down_hops:
            hop_copy(buffer, send, recv, False, number).wait_recv()
            if number < down_hops:
                hop_copy(buffer, send, recv, False, number + 1).start()
        for member in hop_members(number):
            for place in (2, 1, 3):
                if (place, member) != both_ways:
                    near_copy(buffer, send_near, recv_near, place, member).start()

    def take_near(buffer, sems, member):
        for place in (1, 2, 3):
            near_copy(buffer, sems[2], sems[3], place, member).wait_recv()

    def end_spread(buffer, sems):
        send, recv, send_near, recv_near = sems
        for number in range(1, up_hops + 1):
            hop_copy(buffer, send, recv, True, number).wait_send()
        for number in range(1, down_hops + 1):
            hop_copy(buffer, send, recv, False, number).wait_send()
        for member in range(members):
            for place in (1, 2, 3):
                near_copy(buffer, send_near, recv_near, place, member).wait_send()

    def add_determinants(member):
        table = jnp.concatenate([tables[place, member] for place in range(4)], axis=1).astype(F32)
        width = table.shape[1]
        amplitude = table[8:9] + table[9:10] + table[10:11]
        orbital = lax.broadcasted_iota(jnp.int32, (NAO, width), 0).astype(F32)
        particle_hot = jnp.concatenate(
            [
                jnp.where(orbital == table[4 + row : 5 + row], 1.0, 0.0).astype(BF16)
                for row in range(MAXEXC)
            ],
            axis=1,
        )
        picked = jnp.dot(active[:, 0:NAV], particle_hot, preferred_element_type=F32)
        masks = [orbital == table[column : column + 1] for column in range(MAXEXC)]
        pieces = []
        for walker in range(2):
            rows = slice(walker * NAO, (walker + 1) * NAO)
            matrix = []
            for row in range(MAXEXC):
                own = picked[rows, row * width : (row + 1) * width]
                entries = [
                    jnp.sum(jnp.where(masks[column], own, 0.0), axis=0, keepdims=True)
                    for column in range(MAXEXC)
                ]
                entries[row] = jnp.where(table[4 + row : 5 + row] < 0.0, 1.0, entries[row])
                matrix.append(entries)
            ratios, pullback = jax.vjp(minor_determinant, matrix)
            cofactors = pullback(jnp.ones_like(ratios))[0]
            corr_total[walker] += ratios * amplitude
            uppers, lowers = [], []
            for row in range(MAXEXC):
                spread = jnp.zeros((NAO, width), F32)
                for column in range(MAXEXC):
                    spread = jnp.where(masks[column], cofactors[row][column] * amplitude, spread)
                upper = spread.astype(BF16)
                uppers.append(upper)
                lowers.append((spread - upper.astype(F32)).astype(BF16))
            pieces += [jnp.concatenate(uppers, axis=1), jnp.concatenate(lowers, axis=1)]
        grad_total[:, 0:NAV] += transposed_dot(jnp.concatenate(pieces, axis=0), particle_hot)

    def finish_gradient():
        for walker in range(2):
            start = 2 * walker * NAO
            whole = grad_total[start : start + NAO, :] + grad_total[start + NAO : start + 2 * NAO, :]
            packed = whole[0 : NAO // 2] + pltpu.roll(whole[NAO // 2 : NAO], NAV, 1)
            gradients[0, 0, walker] = packed.astype(BF16)

    def add_active(member):
        lanes = lax.broadcasted_iota(jnp.int32, (NAO // 2, 128), 1)
        unpacked = []
        for place in range(4):
            for walker in range(2):
                packed = gradients[place, member, walker].astype(F32)
                unpacked.append(
                    (
                        jnp.where(lanes < NAV, packed, 0.0).astype(BF16),
                        jnp.where(lanes < NAV, pltpu.roll(packed, NAV, 1), 0.0).astype(BF16),
                    )
                )
        for block in range(NAO // BLOCK):
            left = active_chol[pl.ds(block * BLOCK, BLOCK)].reshape(BLOCK * vectors, 128)
            side, inner = divmod(block * BLOCK, NAO // 2)
            right = jnp.concatenate(
                [halves[side][inner : inner + BLOCK] for halves in unpacked], axis=0
            )
            total[...] += transposed_dot(left, right)
        places = [(shift_of(place, member) + STRIDE * member_of(place, member)) % chips for place in range(4)]
        keep_rows(places)
        for place in places:
            if place:
                back_copy(place).start()

    table_sems = (table_send, table_recv, table_send_near, table_recv_near)
    grad_sems = (grad_send, grad_recv, grad_send_near, grad_recv_near)

    def lower_core():
        chol_part = pltpu.make_async_copy(
            chol_ref.at[pl.ds(NOCC - NAO, NAO), :, pl.ds(0, 128)], active_chol, chol_sem.at[0]
        )
        chol_part.start()
        partners = (1, -1, 2, -2, STRIDE, -STRIDE)
        greet(partners, 1)
        own_walker(0)
        order = order_ref[...]
        live = lax.broadcasted_iota(jnp.int32, (MAXEXC, order.shape[1]), 0) < order
        table_build[...] = jnp.zeros_like(table_build)
        table_build[0:4, :] = jnp.where(live, hole_ref[...], -1).astype(F32)
        table_build[4:8, :] = jnp.where(live, particle_ref[...], -1).astype(F32)
        amp = amp_ref[...]
        high = amp.astype(BF16).astype(F32)
        middle = (amp - high).astype(BF16).astype(F32)
        table_build[8:9, :] = high
        table_build[9:10, :] = middle
        table_build[10:11, :] = amp - high - middle
        tables[0, 0] = table_build[...].astype(BF16)

        pl.semaphore_wait(barrier, len(partners) + 1)
        for part in LAST_DOWN:
            block_to_upper(part).start()
        start_spread(tables, table_sems)

        total[...] = jnp.zeros_like(total)
        grad_total[...] = jnp.zeros_like(grad_total)
        corr_total[...] = jnp.zeros_like(corr_total)
        shift_rows = lax.broadcasted_iota(jnp.int32, (NAO, ROWS // 2), 0)
        shift_columns = lax.broadcasted_iota(jnp.int32, (NAO, ROWS // 2), 1)
        offset = NOCC - NAO - ROWS // 2
        shift = (shift_columns == shift_rows + offset).astype(F32).astype(BF16)
        active[0:NAO, :] = jnp.dot(
            shift, greens[0, 0, ROWS // 2 : ROWS, 0:128], preferred_element_type=F32
        ).astype(BF16)
        rows_to_lower().wait_recv()
        active[NAO : 2 * NAO, :] = jnp.dot(
            shift, peer_rows[...], preferred_element_type=F32
        ).astype(BF16)

        late = [0]
        for number in range(1, up_hops + 1):
            take_hop(tables, table_sems, number)
            for member in late:
                take_near(tables, table_sems, member)
                add_determinants(member)
            late = hop_members(number)
        for member in late:
            take_near(tables, table_sems, member)
            add_determinants(member)
        finish_gradient()
        start_spread(gradients, grad_sems)

        for walker in range(2):
            corr_out[walker : walker + 1, :] = jnp.broadcast_to(
                1.0 + jnp.sum(corr_total[walker], axis=1, keepdims=True), (1, 128)
            )
        chol_part.wait()

        late = [0]
        for number in range(1, up_hops + 1):
            take_hop(gradients, grad_sems, number)
            if number == 1:
                corr_to_upper().start()
            for member in late:
                take_near(gradients, grad_sems, member)
                add_active(member)
            late = hop_members(number)
        for member in late:
            take_near(gradients, grad_sems, member)
            add_active(member)
        inbox[lax.rem(me, 2), lax.div(me, 2)] = message[0]

        end_spread(tables, table_sems)
        end_spread(gradients, grad_sems)
        for part in LAST_DOWN:
            block_to_upper(part).wait_send()
        corr_to_upper().wait_send()
        for offset in range(1, chips):
            back_copy(offset).wait_send()
        for offset in range(1, chips):
            back_wait(offset)
        inbox_swap(1).start()
        inbox_swap(1).wait()
        write_bias(corr_out[0:1, 0:1], peer_inbox[...], inbox[...], False)

    @pl.when(core == 1)
    def _():
        upper_core()

    @pl.when(core == 0)
    def _():
        lower_core()


def shards(greens, chol_vectors, hole_orbitals, particle_orbitals, excitation_order, amplitudes):
    chips = lax.axis_size("det")
    vectors = chol_vectors.shape[0]
    dets = hole_orbitals.shape[0]
    members = chips // STRIDE
    half = chips // 2
    dma = pltpu.SemaphoreType.DMA
    vmem = pl.BlockSpec(memory_space=pltpu.VMEM)
    corr, bias = pl.pallas_call(
        functools.partial(kernel, chips),
        out_shape=(
            jax.ShapeDtypeStruct((1, 128), F32),
            jax.ShapeDtypeStruct((chips * vectors // 128, 128), F32),
        ),
        in_specs=[vmem, pl.BlockSpec(memory_space=pl.ANY), vmem, vmem, vmem, vmem],
        out_specs=(vmem, vmem),
        scratch_shapes=[
            pltpu.VMEM((NOCC, vectors, NVIR), BF16),
            pltpu.VMEM((ROWS, vectors, LANES), BF16),
            pltpu.VMEM((NAO, vectors, 128), BF16),
            pltpu.VMEM((chips, 2, ROWS, LANES), BF16),
            pltpu.VMEM((BLOCK * vectors, BATCH * BLOCK), F32),
            pltpu.VMEM((4, members, 16, dets), BF16),
            pltpu.VMEM((4, members, 2, NAO // 2, 128), BF16),
            pltpu.VMEM((16, dets), F32),
            pltpu.VMEM((ROWS // 2, 128), BF16),
            pltpu.VMEM((2 * NAO, 128), BF16),
            pltpu.VMEM((4 * NAO, 128), F32),
            pltpu.VMEM((2, 1, 4 * dets), F32),
            pltpu.VMEM((chips, 1, 128), F32),
            pltpu.VMEM((2, half, 1, 128), F32),
            pltpu.VMEM((2, half, 1, 128), F32),
            pltpu.VMEM((8, 128), F32),
            pltpu.VMEM((8, 128), F32),
            pltpu.VMEM((256, 384), BF16),
            pltpu.VMEM((LAST[1], vectors, 128), F32),
            dma((BLOCKS,)),
            dma((4 + len(CHUNKS) // 2,)),
            dma((4 + len(CHUNKS) // 2,)),
            dma((2, half + 1, len(CHUNKS))),
            dma((2, half + 1, len(CHUNKS))),
            dma((members,)),
            dma((members,)),
            dma((4, members)),
            dma((4, members)),
            dma((members,)),
            dma((members,)),
            dma((4, members)),
            dma((4, members)),
            dma((chips,)),
            dma((chips,)),
        ],
        compiler_params=pltpu.CompilerParams(
            collective_id=0, has_side_effects=True, vmem_limit_bytes=56 * 1024 * 1024
        ),
        name="walker_ring",
    )(
        jnp.transpose(greens, (0, 2, 1)).reshape(NOCC, NVIR),
        jnp.transpose(chol_vectors, (2, 0, 1)),
        jnp.transpose(hole_orbitals),
        jnp.transpose(particle_orbitals),
        excitation_order.reshape(1, dets),
        amplitudes.reshape(1, dets),
    )
    return (corr[0, 0:1], bias.reshape(1, chips * vectors))


def solution(mesh):
    placed = (
        P(("grp", "det", "wlk"), None, None),
        P(("grp", "det"), None, None),
        P(("grp", "det"), None),
        P(("grp", "det"), None),
        P(("grp", "det")),
        P(("grp", "det")),
    )
    return jax.shard_map(
        shards,
        mesh=mesh,
        in_specs=placed,
        out_specs=(P(("grp", "det", "wlk")), P(("grp", "det", "wlk"), None)),
        check_vma=False,
    )
```

time: 318 us -> 113 us (0.36)
  blocking collectives: 113 us -> 0 us
  Pallas kernels: 0 us -> 109 us
  waiting for transfers between devices: 70.8 us -> 0 us
  starting transfers between devices: 49.1 us -> 0 us
  matrix products: 31.8 us -> 0 us
  local copies, waits for them, and re-layouts: 20.3 us -> 1.3 us
  other arithmetic: 16.3 us -> 0 us
  between operations: 16.3 us -> 2.4 us
    psum x1 -> x0, blocking collectives: 113 us -> none  [shards(): lax.psum((gradient_part.reshape(group_walkers, NAV * NAO), correlation_pa...]
    pallas_call x0 -> x1, Pallas kernels: none -> 109 us  [shards(): pl.pallas_call(functools.partial(kernel, chips), out_shape=(jax.ShapeDtyp...]
    all_to_all x3 -> x0, waiting for transfers between devices: 70.2 us -> none  [the longest x1 36.9 us: sent_to_all(): lax.all_to_all(jnp.broadcast_to(value[None], (devices, *value.shape)), ax...]
    all_to_all x3 -> x0, starting transfers between devices: 48.9 us -> none  [the longest x1 32.7 us: sent_to_all(): lax.all_to_all(jnp.broadcast_to(value[None], (devices, *value.shape)), ax...]
    dot_general x8 -> x0, matrix products: 31.8 us -> none  [the longest x1 8.55 us: shards(): lax.dot_general(flat_piece, flat_chol, (((1,), (1,)), ((), ())), preferre...]
    convert_element_type x4 -> x0, other arithmetic: 12.2 us -> none  [the longest x2 11.8 us: split_product(): lower_part = (values - upper_part.astype(jnp.float32)).astype(jnp.bfloat16)]
    convert_element_type x2 -> x0, local copies, waits for them, and re-layouts: 6.87 us -> none  [the longest x1 6.43 us: block_terms(): picked_rows = jnp.einsum('dja,wai->wdji', particle_hot, active_green, pre...]
    unnamed x13 -> x1, local copies, waits for them, and re-layouts: 4.75 us -> 1.3 us
  transfers between devices with their start and end apart: 4 -> 0, of which waited for: 3 -> 0; matrix products, arithmetic and copies ran while one was open for 19% -> 0% of each run, Pallas kernels for 0% -> 0%
where the time goes in v2:
time: 113 us; the launch traced here: 112 us
  Pallas kernels  109 us (96%)
  between operations  2.4 us (2%)
  local copies, waits for them, and re-layouts  1.3 us (1%)
    pallas_call x1, Pallas kernels, shards(): pl.pallas_call(functools.partial(kernel, chips), out_shape=(jax.ShapeDtyp...  109 us

profile of v2, /device:TPU:38, one launch (start us, length us, event | category | flops | bytes accessed | tf_op | source)
XLA Modules:
  0.0 112.5 jit_solution(586761664967559389)
XLA Ops:
  0.6 108.8 %walker_ring.1 = (f32[1,128]{1,0:T(1,128)}, f32[16,128]{1,0:T(8,128)}) custom-call(bf16[150,450]{1,0:T(8,128)(2,1)} %bitcast.12, bf16[150,64,450]{2,1,0:T(8,128)(2,1)} %bitcast.11, s32[4,128]{1,0:T(4,128)} %bitcast.14, s32[4,128]{1,0:T(4,128)} %bitcast.15, s32[1,128]{1,0:T(1,128)} %bitcast.16, f32[1,128]{1,0:T(1,128)} %bitcast.17), custom_call_target="tpu_custom_call" | custom-call | tf_op jit(solution)/shard_map/walker_ring/pallas_call | solution.py:685
  110.0 1.3 %copy.11 = f32[1,2048]{1,0:T(1,128)} copy(f32[1,2048]{1,0:T(1,128)} %bitcast.13) | data formatting | bytes 16384

commit v3 on v2

--- a/solution.py
+++ b/solution.py
@@ -112,6 +112,8 @@
     grad_recv_near,
     back_send,
     back_recv,
+    near_sem,
+    far_sem,
 ):
     half = chips // 2
     members = chips // STRIDE
@@ -583,9 +585,14 @@
             chol_ref.at[pl.ds(NOCC - NAO, NAO), :, pl.ds(0, 128)], active_chol, chol_sem.at[0]
         )
         chol_part.start()
-        partners = (1, -1, 2, -2, STRIDE, -STRIDE)
-        greet(partners, 1)
+        greet((1, -1), 1)
         own_walker(0)
+        pl.semaphore_wait(barrier, 3)
+        for part in LAST_DOWN:
+            block_to_upper(part).start()
+        for offset in (1, -1):
+            pl.semaphore_signal(near_sem, inc=1, device_id=chip(offset), device_id_type=MESH)
+
         order = order_ref[...]
         live = lax.broadcasted_iota(jnp.int32, (MAXEXC, order.shape[1]), 0) < order
         table_build[...] = jnp.zeros_like(table_build)
@@ -599,9 +606,10 @@
         table_build[10:11, :] = amp - high - middle
         tables[0, 0] = table_build[...].astype(BF16)
 
-        pl.semaphore_wait(barrier, len(partners) + 1)
-        for part in LAST_DOWN:
-            block_to_upper(part).start()
+        pl.semaphore_wait(near_sem, 2)
+        for offset in (2, -2):
+            pl.semaphore_signal(far_sem, inc=1, device_id=chip(offset), device_id_type=MESH)
+        pl.semaphore_wait(far_sem, 2)
         start_spread(tables, table_sems)
 
         total[...] = jnp.zeros_like(total)
@@ -725,6 +733,8 @@
             dma((4, members)),
             dma((chips,)),
             dma((chips,)),
+            pltpu.SemaphoreType.REGULAR,
+            pltpu.SemaphoreType.REGULAR,
         ],
         compiler_params=pltpu.CompilerParams(
             collective_id=0, has_side_effects=True, vmem_limit_bytes=56 * 1024 * 1024

time: 113 us -> 111 us (0.982)
  Pallas kernels: 109 us -> 107 us
    pallas_call x1, Pallas kernels: 109 us -> 107 us  [shards(): pl.pallas_call(functools.partial(kernel, chips), out_shape=(jax.ShapeDtyp...]
where the time goes in v3:
time: 111 us
  Pallas kernels  107 us (96%)
  between operations  2.4 us (2%)
  local copies, waits for them, and re-layouts  1.3 us (1%)
    pallas_call x1, Pallas kernels, shards(): pl.pallas_call(functools.partial(kernel, chips), out_shape=(jax.ShapeDtyp...  107 us

profile of v3, /device:TPU:38, one launch (start us, length us, event | category | flops | bytes accessed | tf_op | source)
XLA Modules:
  0.0 110.5 jit_solution(2088153044320176405)
XLA Ops:
  0.6 106.8 %walker_ring.1 = (f32[1,128]{1,0:T(1,128)}, f32[16,128]{1,0:T(8,128)}) custom-call(bf16[150,450]{1,0:T(8,128)(2,1)} %bitcast.12, bf16[150,64,450]{2,1,0:T(8,128)(2,1)} %bitcast.11, s32[4,128]{1,0:T(4,128)} %bitcast.14, s32[4,128]{1,0:T(4,128)} %bitcast.15, s32[1,128]{1,0:T(1,128)} %bitcast.16, f32[1,128]{1,0:T(1,128)} %bitcast.17), custom_call_target="tpu_custom_call" | custom-call | tf_op jit(solution)/shard_map/walker_ring/pallas_call | solution.py:693
  108.1 1.3 %copy.11 = f32[1,2048]{1,0:T(1,128)} copy(f32[1,2048]{1,0:T(1,128)} %bitcast.13) | data formatting | bytes 16384

commit v4 on v3

--- a/solution.py
+++ b/solution.py
@@ -112,6 +112,8 @@
     grad_recv_near,
     back_send,
     back_recv,
+    lower_send,
+    lower_recv,
     near_sem,
     far_sem,
 ):
@@ -164,6 +166,27 @@
             device_id={"det": lax.rem(me - offset + chips, chips)},
             device_id_type=MESH,
         )
+
+    def back_copy_lower(offset):
+        return pltpu.make_async_remote_copy(
+            src_ref=message.at[offset],
+            dst_ref=peer_inbox.at[lax.rem(me, 2), lax.div(me, 2)],
+            send_sem=lower_send.at[offset],
+            recv_sem=lower_recv.at[offset],
+            device_id={"det": lax.rem(me - offset + chips, chips), "wlk": 0},
+            device_id_type=MESH,
+        )
+
+    def back_wait_lower(offset):
+        sender = lax.rem(me + offset, chips)
+        pltpu.make_async_remote_copy(
+            src_ref=message.at[offset],
+            dst_ref=peer_inbox.at[lax.rem(sender, 2), lax.div(sender, 2)],
+            send_sem=lower_send.at[offset],
+            recv_sem=lower_recv.at[offset],
+            device_id={"det": sender, "wlk": 1},
+            device_id_type=MESH,
+        ).wait_recv()
 
     def back_wait(offset):
         sender = lax.rem(me + offset, chips)
@@ -385,6 +408,7 @@
                 keep_rows(places)
                 for place in places:
                     back_copy(place).start()
+                    back_copy_lower(place).start()
 
         step = half - 1
         slots = (half - 3, half - 2, 2 * half - 3, 2 * half - 2)
@@ -396,6 +420,7 @@
         keep_rows(places)
         for place in places:
             back_copy(place).start()
+            back_copy_lower(place).start()
 
         slots = (half, half - 1, 2 * half - 1, 0)
         for part in range(len(CHUNKS)):
@@ -404,7 +429,9 @@
                 add_block(slots, block)
         keep_rows((half, half - 1, half + 1, 0))
         for place in (half, half - 1, half + 1):
+            back_copy_lower(place).start()
             back_copy(place).start()
+        back_copy_lower(0).start()
         inbox[lax.rem(me, 2), lax.div(me, 2)] = message[0]
 
         rows_to_lower().wait_send()
@@ -426,9 +453,9 @@
             back_copy(offset).wait_send()
         for offset in range(1, chips):
             back_wait(offset)
-        inbox_swap(0).start()
         write_bias(corr_in[1:2, 0:1], inbox[...], peer_inbox[...], True)
-        inbox_swap(0).wait_send()
+        for offset in range(chips):
+            back_copy_lower(offset).wait_send()
 
     up_hops = members // 2
     down_hops = members - 1 - up_hops
@@ -670,7 +697,9 @@
         for offset in range(1, chips):
             back_wait(offset)
         inbox_swap(1).start()
-        inbox_swap(1).wait()
+        inbox_swap(1).wait_send()
+        for offset in range(chips):
+            back_wait_lower(offset)
         write_bias(corr_out[0:1, 0:1], peer_inbox[...], inbox[...], False)
 
     @pl.when(core == 1)
@@ -733,6 +762,8 @@
             dma((4, members)),
             dma((chips,)),
             dma((chips,)),
+            dma((chips,)),
+            dma((chips,)),
             pltpu.SemaphoreType.REGULAR,
             pltpu.SemaphoreType.REGULAR,
         ],

time: 111 us -> 112 us (level)
  no operation moved by 1% of the time
where the time goes in v4:
time: 112 us; the launch traced here: 111 us
  Pallas kernels  107 us (96%)
  between operations  2.4 us (2%)
  local copies, waits for them, and re-layouts  1.3 us (1%)
    pallas_call x1, Pallas kernels, shards(): pl.pallas_call(functools.partial(kernel, chips), out_shape=(jax.ShapeDtyp...  107 us

profile of v4, /device:TPU:38, one launch (start us, length us, event | category | flops | bytes accessed | tf_op | source)
XLA Modules:
  0.0 111.1 jit_solution(18151287664350412812)
XLA Ops:
  0.6 107.4 %walker_ring.1 = (f32[1,128]{1,0:T(1,128)}, f32[16,128]{1,0:T(8,128)}) custom-call(bf16[150,450]{1,0:T(8,128)(2,1)} %bitcast.12, bf16[150,64,450]{2,1,0:T(8,128)(2,1)} %bitcast.11, s32[4,128]{1,0:T(4,128)} %bitcast.14, s32[4,128]{1,0:T(4,128)} %bitcast.15, s32[1,128]{1,0:T(1,128)} %bitcast.16, f32[1,128]{1,0:T(1,128)} %bitcast.17), custom_call_target="tpu_custom_call" | custom-call | tf_op jit(solution)/shard_map/walker_ring/pallas_call | solution.py:722
  108.7 1.3 %copy.11 = f32[1,2048]{1,0:T(1,128)} copy(f32[1,2048]{1,0:T(1,128)} %bitcast.13) | data formatting | bytes 16384
